TPU v7x, 32 devices: a whole 2x2x4 slice. The times are simulated.
32 devices in a mesh: hi: 4 (over z), lo: 8 (over y, x, core).
Axes of the slice: x: 2, y: 2, z: 4, core: 2. Of those that a mesh axis runs over, the one named last changes fastest.
Arguments:
- state: float32 [2, 33554432], P(None, ('hi', 'lo')), may hold values from -6 to 6
Outputs:
- transformed: float32 [2, 33554432], P(None, ('hi', 'lo'))
All inputs are finite; a program needn't handle non-finite values.
Results may differ from a plain program's by a relative error of at most 0.0003.
Values sent between devices are 32-bit elements.
A program may use at most 128 MiB of HBM per device.

v0:
```python
import math
import jax
import jax.numpy as jnp
from jax import lax
from jax.sharding import PartitionSpec as P

SUB_A = 1024


def product(left, right):
    return jnp.dot(left, right, precision=lax.Precision.HIGHEST, preferred_element_type=jnp.float32)


def dft_table(length, factor):
    steps = jnp.arange(length, dtype=jnp.int32)
    indices = steps[:, None] * steps[None, :] % length
    phases = indices.astype(jnp.float32) * (2.0 * math.pi / length)
    return (jnp.cos(phases) * factor, jnp.sin(phases) * factor)


def rotate(real_part, imag_part, phases):
    cosine = jnp.cos(phases)
    sine = jnp.sin(phases)
    return (real_part * cosine - imag_part * sine, real_part * sine + imag_part * cosine)


def remap_entry(blocks):
    return lax.all_to_all(blocks, ("hi", "lo"), split_axis=1, concat_axis=1, tiled=True)


def remap_middle(blocks):
    return lax.all_to_all(blocks, ("hi", "lo"), split_axis=1, concat_axis=1, tiled=True)


def remap_final(blocks):
    return lax.all_to_all(blocks, ("hi", "lo"), split_axis=1, concat_axis=1, tiled=True)


def shards(state):
    count_high = lax.axis_size("hi")
    count_low = lax.axis_size("lo")
    devices_all = count_high * count_low
    device_pos = lax.axis_index("hi") * count_low + lax.axis_index("lo")
    amplitudes = state.shape[1]
    per_peer = amplitudes // devices_all
    whole_size = amplitudes * devices_all
    blocks = remap_entry(state.reshape(2, devices_all, per_peer))
    table_re, table_im = dft_table(devices_all, 1.0 / math.sqrt(devices_all))
    mixed_re = product(table_re, blocks[0]) - product(table_im, blocks[1])
    mixed_im = product(table_re, blocks[1]) + product(table_im, blocks[0])
    row_ids = jnp.arange(devices_all, dtype=jnp.int32)
    col_ids = device_pos * per_peer + jnp.arange(per_peer, dtype=jnp.int32)
    phases = (row_ids[:, None] * col_ids[None, :] % whole_size).astype(jnp.float32) * (
        2.0 * math.pi / whole_size
    )
    mixed_re, mixed_im = rotate(mixed_re, mixed_im, phases)
    gathered = remap_middle(jnp.stack([mixed_re, mixed_im]))
    outer_len = SUB_A
    inner_len = amplitudes // outer_len
    local_grid = gathered.reshape(2, outer_len, inner_len)
    outer_re, outer_im = dft_table(outer_len, 1.0 / math.sqrt(outer_len))
    half_re = product(outer_re, local_grid[0]) - product(outer_im, local_grid[1])
    half_im = product(outer_re, local_grid[1]) + product(outer_im, local_grid[0])
    outer_ids = jnp.arange(outer_len, dtype=jnp.int32)
    inner_ids = jnp.arange(inner_len, dtype=jnp.int32)
    phases = (outer_ids[:, None] * inner_ids[None, :] % amplitudes).astype(jnp.float32) * (
        2.0 * math.pi / amplitudes
    )
    half_re, half_im = rotate(half_re, half_im, phases)
    inner_re, inner_im = dft_table(inner_len, 1.0 / math.sqrt(inner_len))
    done_re = product(half_re, inner_re) - product(half_im, inner_im)
    done_im = product(half_re, inner_im) + product(half_im, inner_re)
    ordered = jnp.stack([done_re, done_im]).transpose(0, 2, 1).reshape(2, devices_all, per_peer)
    arrived = remap_final(ordered)
    return arrived.transpose(0, 2, 1).reshape(2, amplitudes)


def solution(mesh):
    placed = (P(None, ("hi", "lo")),)
    return jax.shard_map(
        shards, mesh=mesh, in_specs=placed, out_specs=P(None, ("hi", "lo")), check_vma=False
    )
```

profile of v0, /device:TPU:0, one launch (start us, length us, event | category | flops | bytes accessed | tf_op | source)
XLA Modules:
  0.0 1071.1 jit_solution(11624295385155374427)
XLA Ops:
  0.0 7.5 all-to-all-start
  7.5 185.9 %all-to-all-done = f32[2,32,32768]{2,0,1:T(2,128)} async-done(((f32[2,32,32768]{2,0,1:T(2,128)}), f32[2,32,32768]{2,0,1:T(2,128)}, u32[]{:S(2)}, u32[]{:S(2)}) %all-to-all-start) | async-done | bytes 8388640 | tf_op jit(solution)/shard_map/all_to_all | solution.py:28
  193.4 9.9 fusion.143
  203.2 5.9 fusion.11
  209.1 5.9 fusion.7
  215.0 6.1 convolution_add_fusion
  221.1 22.9 %subtract_bitcast_fusion.1 = (f32[1,32,32768]{2,1,0:T(8,128)S(1)}, f32[1,32,32768]{2,1,0:T(8,128)S(1)}) fusion(f32[32,32768]{1,0:T(8,128)S(1)} %convolution_add_fusion, s32[32768]{0:T(1024)S(1)} %iota_add_fusion, f32[32,32768]{1,0:T(8,128)S(1)} %fusion.11, f32[1,32,32768]{2,0,1:T(1,128)S(1)} %get-tuple-element.10), kind=kOutput, calls=%fused_computation.33 | convolution fusion | flops 424688640 | bytes 21102592 | tf_op jit(solution)/shard_map/dot_general | solution.py:11
  244.1 0.5 pad_maximum_fusion
  244.6 14.3 %copy.4 = f32[2,32,32768]{2,0,1:T(2,128)S(1)} copy(f32[2,32,32768]{2,1,0:T(8,128)S(1)} %pad_maximum_fusion) | data formatting | bytes 16777216 | tf_op jit(solution)/shard_map/stack | solution.py:57
  258.9 186.0 %all_to_all.15 = f32[2,32,32768]{2,0,1:T(2,128)} all-to-all(f32[2,32,32768]{2,0,1:T(2,128)S(1)} %copy.4), channel_id=1, replica_groups=mesh['hi'=4,'lo'=8] {'hi','lo'}, dimensions={1} | all-to-all | bytes 16777216 | tf_op jit(solution)/shard_map/all_to_all | solution.py:32
  444.9 28.8 %slice_reduce_fusion.1 = (f32[32,32768]{1,0:T(8,128)}, f32[32,32768]{1,0:T(8,128)}) fusion(f32[2,32,32768]{2,0,1:T(2,128)} %all_to_all.15), kind=kLoop, calls=%fused_computation.20 | loop fusion | bytes 16777216 | tf_op jit(solution)/shard_map/slice | solution.py:62
  473.7 4.9 squeeze.18
  478.7 4.9 squeeze.19
  483.6 31.5 %fusion.29 = f32[1024,1024]{1,0:T(8,128)S(1)} fusion(f32[1024,1024]{1,0:T(8,128)} %squeeze.19), kind=kOutput, calls=%fused_computation.52 | convolution fusion | flops 12900630528 | bytes 8388608 | tf_op jit(solution)/shard_map/dot_general | solution.py:11
  515.2 29.6 %fusion.30 = f32[1024,1024]{1,0:T(8,128)S(1)} fusion(f32[1024,1024]{1,0:T(8,128)S(1)} %copy-done), kind=kOutput, calls=%fused_computation.53 | convolution fusion | flops 12900630528 | bytes 8388608 | tf_op jit(solution)/shard_map/dot_general | solution.py:11
  544.8 29.2 %fusion.56 = f32[1024,1024]{1,0:T(8,128)S(1)} fusion(f32[1024,1024]{1,0:T(8,128)S(1)} %fusion.29, f32[1024,1024]{1,0:T(8,128)S(1)} %copy-done), kind=kOutput, calls=%fused_computation.71 | convolution fusion | flops 12901679104 | bytes 12582912 | tf_op jit(solution)/shard_map/dot_general | solution.py:11
  574.0 29.7 %fusion.55 = f32[1024,1024]{1,0:T(8,128)S(1)} fusion(f32[1024,1024]{1,0:T(8,128)S(1)} %fusion.30, f32[1024,1024]{1,0:T(8,128)S(1)} %copy-done.1), kind=kOutput, calls=%fused_computation.70 | convolution fusion | flops 12901679104 | bytes 12582912 | tf_op jit(solution)/shard_map/dot_general | solution.py:11
  603.7 16.8 %multiply_add_fusion.10 = f32[1024,1024]{1,0:T(8,128)S(1)} fusion(f32[1024,1024]{1,0:T(8,128)S(1)} %fusion.56, f32[1024,1024]{1,0:T(8,128)S(1)} %fusion.55), kind=kLoop, calls=%fused_computation.29.clone.clone.2 | loop fusion | flops 17825792 | bytes 12582912 | tf_op jit(solution)/shard_map/dot_general | solution.py:11
  620.6 16.8 %multiply_subtract_fusion.9 = f32[1024,1024]{1,0:T(8,128)S(1)} fusion(f32[1024,1024]{1,0:T(8,128)S(1)} %fusion.56, f32[1024,1024]{1,0:T(8,128)S(1)} %fusion.55), kind=kLoop, calls=%fused_computation.30.clone.clone.2 | loop fusion | flops 17825792 | bytes 12582912 | tf_op jit(solution)/shard_map/dot_general | solution.py:11
  637.4 16.8 %multiply_add_fusion.9 = f32[1024,1024]{1,0:T(8,128)S(1)} fusion(f32[1024,1024]{1,0:T(8,128)S(1)} %fusion.56, f32[1024,1024]{1,0:T(8,128)S(1)} %fusion.55), kind=kLoop, calls=%fused_computation.29.clone.1.clone.2 | loop fusion | flops 17825792 | bytes 12582912 | tf_op jit(solution)/shard_map/dot_general | solution.py:11
  654.2 16.8 %multiply_subtract_fusion.10 = f32[1024,1024]{1,0:T(8,128)S(1)} fusion(f32[1024,1024]{1,0:T(8,128)S(1)} %fusion.56, f32[1024,1024]{1,0:T(8,128)S(1)} %fusion.55), kind=kLoop, calls=%fused_computation.30.clone.1.clone.2 | loop fusion | flops 17825792 | bytes 12582912 | tf_op jit(solution)/shard_map/dot_general | solution.py:11
  671.1 31.3 %fusion.27 = f32[1024,1024]{1,0:T(8,128)S(1)} fusion(f32[1024,1024]{1,0:T(8,128)S(1)} %multiply_add_fusion.10), kind=kOutput, calls=%fused_computation.50 | convolution fusion | flops 12900630528 | bytes 8388608 | tf_op jit(solution)/shard_map/dot_general | solution.py:11
  702.4 31.4 %fusion.28 = f32[1024,1024]{1,0:T(8,128)S(1)} fusion(f32[1024,1024]{1,0:T(8,128)S(1)} %multiply_subtract_fusion.10), kind=kOutput, calls=%fused_computation.51 | convolution fusion | flops 12900630528 | bytes 8388608 | tf_op jit(solution)/shard_map/dot_general | solution.py:11
  733.8 31.5 %add_bitcast_fusion = f32[1,1024,1024]{2,1,0:T(8,128)S(1)} fusion(f32[1024,1024]{1,0:T(8,128)S(1)} %fusion.27, f32[1024,1024]{1,0:T(8,128)S(1)} %multiply_subtract_fusion.9), kind=kOutput, calls=%fused_computation.27 | convolution fusion | flops 12901679104 | bytes 12582912 | tf_op jit(solution)/shard_map/dot_general | solution.py:11
  765.3 31.3 %subtract_bitcast_fusion = f32[1,1024,1024]{2,1,0:T(8,128)S(1)} fusion(f32[1024,1024]{1,0:T(8,128)S(1)} %fusion.28, f32[1024,1024]{1,0:T(8,128)S(1)} %multiply_add_fusion.9), kind=kOutput, calls=%fused_computation.28 | convolution fusion | flops 12901679104 | bytes 12582912 | tf_op jit(solution)/shard_map/dot_general | solution.py:11
  796.6 4.2 maximum_bitcast_fusion
  800.8 8.7 copy.5
  809.5 9.4 reshape.19
  818.9 14.4 %copy.6 = f32[2,32,32768]{2,0,1:T(2,128)S(1)} copy(f32[2,32,32768]{2,1,0:T(8,128)} %reshape.19) | data formatting | bytes 16777216 | tf_op jit(solution)/shard_map/reshape | solution.py:73
  833.3 187.3 %all_to_all.16 = f32[2,32,32768]{2,0,1:T(2,128)} all-to-all(f32[2,32,32768]{2,0,1:T(2,128)S(1)} %copy.6), channel_id=1, replica_groups=mesh['hi'=4,'lo'=8] {'hi','lo'}, dimensions={1} | all-to-all | bytes 16777216 | tf_op jit(solution)/shard_map/all_to_all | solution.py:36
  1020.6 22.5 %copy.7 = f32[2,32768,32]{2,1,0:T(8,128)} copy(f32[2,32768,32]{1,0,2:T(2,128)} %bitcast.36) | data formatting | bytes 16777216 | tf_op jit(solution)/shard_map/transpose | solution.py:75
  1043.1 27.8 %reshape.20 = f32[2,1048576]{1,0:T(2,128)} reshape(f32[2,32768,32]{2,1,0:T(8,128)} %copy.7) | data formatting | bytes 16777216 | tf_op jit(solution)/shard_map/reshape | solution.py:75
  (5 shorter events, 0.0 us)
Async XLA Ops:
  0.0 193.4 %all-to-all-start = ((f32[2,32,32768]{2,0,1:T(2,128)}), f32[2,32,32768]{2,0,1:T(2,128)}, u32[]{:S(2)}, u32[]{:S(2)}) async-start(f32[2,32,32768]{2,0,1:T(2,128)} %bitcast.37), calls=%async_computation | async-start | bytes 16777216 | tf_op jit(solution)/shard_map/all_to_all | solution.py:28
  483.6 31.6 %copy-start = (f32[1024,1024]{1,0:T(8,128)S(1)}, f32[1024,1024]{1,0:T(8,128)}, u32[]{:S(2)}) copy-start(f32[1024,1024]{1,0:T(8,128)} %squeeze.18) | copy-start | bytes 12582916
  544.8 29.2 %copy-start.1 = (f32[1024,1024]{1,0:T(8,128)S(1)}, f32[1024,1024]{1,0:T(8,128)}, u32[]{:S(2)}) copy-start(f32[1024,1024]{1,0:T(8,128)} %squeeze.19) | copy-start | bytes 12582916
where the time goes:
time: 1080 us; the launch traced here: 1070 us
  blocking collectives  373 us (35%)
  matrix products  286 us (26%)
  waiting for transfers between devices  186 us (17%)
  local copies, waits for them, and re-layouts  146 us (14%)
  other arithmetic  72.1 us (7%)
    dot_general x12, matrix products, product(): jnp.dot(left, right, precision=lax.Precision.HIGHEST, preferred_element_t...  286 us
    all_to_all x1, blocking collectives, remap_final(): lax.all_to_all(blocks, ('hi', 'lo'), split_axis=1, concat_axis=1, tiled=T...  187 us
    all_to_all x1, blocking collectives, remap_middle(): lax.all_to_all(blocks, ('hi', 'lo'), split_axis=1, concat_axis=1, tiled=T...  186 us
    all_to_all x1, waiting for transfers between devices, remap_entry(): lax.all_to_all(blocks, ('hi', 'lo'), split_axis=1, concat_axis=1, tiled=T...  186 us
    dot_general x4, other arithmetic, product(): jnp.dot(left, right, precision=lax.Precision.HIGHEST, preferred_element_t...  67.3 us
    slice x1, local copies, waits for them, and re-layouts, shards(): local_grid[0]  28.8 us
    reshape x1, local copies, waits for them, and re-layouts, shards(): return arrived.transpose(0, 2, 1).reshape(2, amplitudes)  27.8 us
    reshape x2, local copies, waits for them, and re-layouts, shards(): jnp.stack([done_re, done_im]).transpose(0, 2, 1)  23.7 us
  transfers between devices with their start and end apart: 1, of which 1 were waited for; matrix products, arithmetic and copies ran while one was open for 0% of the time, Pallas kernels for 0%

commit v1 on v0

--- a/solution.py
+++ b/solution.py
@@ -33,7 +33,12 @@
 
 
 def remap_final(blocks):
-    return lax.all_to_all(blocks, ("hi", "lo"), split_axis=1, concat_axis=1, tiled=True)
+    return jnp.concatenate(
+        lax.all_to_all(
+            jnp.stack(jnp.split(blocks, lax.axis_size(("hi", "lo")), axis=1)), ("hi", "lo"), 0, 0
+        ),
+        axis=1,
+    )
 
 
 def shards(state):

time: 1080 us -> 1130 us (1.046)
  local copies, waits for them, and re-layouts: 146 us -> 198 us
    unnamed x4 -> x36, local copies, waits for them, and re-layouts: 0.01 us -> 64.2 us
    reshape x2 -> x1, local copies, waits for them, and re-layouts: 23.7 us -> 9.54 us  [shards(): jnp.stack([done_re, done_im]).transpose(0, 2, 1)]
where the time goes in v1:
time: 1130 us; the launch traced here: 1120 us
  blocking collectives  373 us (33%)
  matrix products  286 us (25%)
  local copies, waits for them, and re-layouts  198 us (18%)
  waiting for transfers between devices  186 us (16%)
  other arithmetic  72.1 us (6%)
    dot_general x12, matrix products, product(): jnp.dot(left, right, precision=lax.Precision.HIGHEST, preferred_element_t...  286 us
    all_to_all x1, blocking collectives, remap_final(): lax.all_to_all(jnp.stack(jnp.split(blocks, lax.axis_size(('hi', 'lo')), a...  187 us
    all_to_all x1, blocking collectives, remap_middle(): lax.all_to_all(blocks, ('hi', 'lo'), split_axis=1, concat_axis=1, tiled=T...  186 us
    all_to_all x1, waiting for transfers between devices, remap_entry(): lax.all_to_all(blocks, ('hi', 'lo'), split_axis=1, concat_axis=1, tiled=T...  186 us
    dot_general x4, other arithmetic, product(): jnp.dot(left, right, precision=lax.Precision.HIGHEST, preferred_element_t...  67.3 us
    unnamed x36, local copies, waits for them, and re-layouts  64.2 us
    slice x1, local copies, waits for them, and re-layouts, shards(): local_grid[0]  28.8 us
    reshape x1, local copies, waits for them, and re-layouts, shards(): return arrived.transpose(0, 2, 1).reshape(2, amplitudes)  27.8 us
  transfers between devices with their start and end apart: 1, of which 1 were waited for; matrix products, arithmetic and copies ran while one was open for 0% of the time, Pallas kernels for 0%

profile of v1, /device:TPU:0, one launch (start us, length us, event | category | flops | bytes accessed | tf_op | source)
XLA Modules:
  0.0 1123.3 jit_solution(8773333840686247937)
XLA Ops:
  0.0 7.5 all-to-all-start
  7.5 185.9 %all-to-all-done = f32[2,32,32768]{2,0,1:T(2,128)} async-done(((f32[2,32,32768]{2,0,1:T(2,128)}), f32[2,32,32768]{2,0,1:T(2,128)}, u32[]{:S(2)}, u32[]{:S(2)}) %all-to-all-start) | async-done | bytes 8388640 | tf_op jit(solution)/shard_map/all_to_all | solution.py:28
  193.4 9.9 fusion.175
  203.2 5.9 fusion.11
  209.1 5.9 fusion.7
  215.0 6.1 convolution_add_fusion
  221.1 23.0 %subtract_bitcast_fusion.1 = (f32[1,32,32768]{2,1,0:T(8,128)S(1)}, f32[1,32,32768]{2,1,0:T(8,128)S(1)}) fusion(f32[32,32768]{1,0:T(8,128)S(1)} %convolution_add_fusion, s32[32768]{0:T(1024)S(1)} %iota_add_fusion, f32[32,32768]{1,0:T(8,128)S(1)} %fusion.11, f32[1,32,32768]{2,0,1:T(1,128)S(1)} %get-tuple-element.10), kind=kOutput, calls=%fused_computation.34 | convolution fusion | flops 424688640 | bytes 21102592 | tf_op jit(solution)/shard_map/dot_general | solution.py:11
  244.7 14.3 %copy.36 = f32[2,32,32768]{2,0,1:T(2,128)S(1)} copy(f32[2,32,32768]{2,1,0:T(8,128)S(1)} %pad_maximum_fusion) | data formatting | bytes 16777216 | tf_op jit(solution)/shard_map/stack | solution.py:62
  259.0 186.0 %all_to_all.15 = f32[2,32,32768]{2,0,1:T(2,128)} all-to-all(f32[2,32,32768]{2,0,1:T(2,128)S(1)} %copy.36), channel_id=1, replica_groups=mesh['hi'=4,'lo'=8] {'hi','lo'}, dimensions={1} | all-to-all | bytes 16777216 | tf_op jit(solution)/shard_map/all_to_all | solution.py:32
  445.0 28.8 %slice_reduce_fusion.1 = (f32[32,32768]{1,0:T(8,128)}, f32[32,32768]{1,0:T(8,128)}) fusion(f32[2,32,32768]{2,0,1:T(2,128)} %all_to_all.15), kind=kLoop, calls=%fused_computation.21 | loop fusion | bytes 16777216 | tf_op jit(solution)/shard_map/slice | solution.py:67
  473.8 4.9 squeeze.18
  478.8 4.9 squeeze.19
  483.7 31.5 %fusion.29 = f32[1024,1024]{1,0:T(8,128)S(1)} fusion(f32[1024,1024]{1,0:T(8,128)} %squeeze.19), kind=kOutput, calls=%fused_computation.53 | convolution fusion | flops 12900630528 | bytes 8388608 | tf_op jit(solution)/shard_map/dot_general | solution.py:11
  515.3 29.6 %fusion.30 = f32[1024,1024]{1,0:T(8,128)S(1)} fusion(f32[1024,1024]{1,0:T(8,128)S(1)} %copy-done), kind=kOutput, calls=%fused_computation.54 | convolution fusion | flops 12900630528 | bytes 8388608 | tf_op jit(solution)/shard_map/dot_general | solution.py:11
  544.9 29.2 %fusion.56 = f32[1024,1024]{1,0:T(8,128)S(1)} fusion(f32[1024,1024]{1,0:T(8,128)S(1)} %fusion.29, f32[1024,1024]{1,0:T(8,128)S(1)} %copy-done), kind=kOutput, calls=%fused_computation.72 | convolution fusion | flops 12901679104 | bytes 12582912 | tf_op jit(solution)/shard_map/dot_general | solution.py:11
  574.1 29.7 %fusion.55 = f32[1024,1024]{1,0:T(8,128)S(1)} fusion(f32[1024,1024]{1,0:T(8,128)S(1)} %fusion.30, f32[1024,1024]{1,0:T(8,128)S(1)} %copy-done.1), kind=kOutput, calls=%fused_computation.71 | convolution fusion | flops 12901679104 | bytes 12582912 | tf_op jit(solution)/shard_map/dot_general | solution.py:11
  603.8 16.8 %multiply_add_fusion.10 = f32[1024,1024]{1,0:T(8,128)S(1)} fusion(f32[1024,1024]{1,0:T(8,128)S(1)} %fusion.56, f32[1024,1024]{1,0:T(8,128)S(1)} %fusion.55), kind=kLoop, calls=%fused_computation.30.clone.clone.2 | loop fusion | flops 17825792 | bytes 12582912 | tf_op jit(solution)/shard_map/dot_general | solution.py:11
  620.7 16.8 %multiply_subtract_fusion.9 = f32[1024,1024]{1,0:T(8,128)S(1)} fusion(f32[1024,1024]{1,0:T(8,128)S(1)} %fusion.56, f32[1024,1024]{1,0:T(8,128)S(1)} %fusion.55), kind=kLoop, calls=%fused_computation.31.clone.clone.2 | loop fusion | flops 17825792 | bytes 12582912 | tf_op jit(solution)/shard_map/dot_general | solution.py:11
  637.5 16.8 %multiply_add_fusion.9 = f32[1024,1024]{1,0:T(8,128)S(1)} fusion(f32[1024,1024]{1,0:T(8,128)S(1)} %fusion.56, f32[1024,1024]{1,0:T(8,128)S(1)} %fusion.55), kind=kLoop, calls=%fused_computation.30.clone.1.clone.2 | loop fusion | flops 17825792 | bytes 12582912 | tf_op jit(solution)/shard_map/dot_general | solution.py:11
  654.3 16.8 %multiply_subtract_fusion.10 = f32[1024,1024]{1,0:T(8,128)S(1)} fusion(f32[1024,1024]{1,0:T(8,128)S(1)} %fusion.56, f32[1024,1024]{1,0:T(8,128)S(1)} %fusion.55), kind=kLoop, calls=%fused_computation.31.clone.1.clone.2 | loop fusion | flops 17825792 | bytes 12582912 | tf_op jit(solution)/shard_map/dot_general | solution.py:11
  671.2 31.3 %fusion.27 = f32[1024,1024]{1,0:T(8,128)S(1)} fusion(f32[1024,1024]{1,0:T(8,128)S(1)} %multiply_add_fusion.10), kind=kOutput, calls=%fused_computation.51 | convolution fusion | flops 12900630528 | bytes 8388608 | tf_op jit(solution)/shard_map/dot_general | solution.py:11
  702.5 31.4 %fusion.28 = f32[1024,1024]{1,0:T(8,128)S(1)} fusion(f32[1024,1024]{1,0:T(8,128)S(1)} %multiply_subtract_fusion.10), kind=kOutput, calls=%fused_computation.52 | convolution fusion | flops 12900630528 | bytes 8388608 | tf_op jit(solution)/shard_map/dot_general | solution.py:11
  733.9 31.5 %add_bitcast_fusion = f32[1,1024,1024]{2,1,0:T(8,128)S(1)} fusion(f32[1024,1024]{1,0:T(8,128)S(1)} %fusion.27, f32[1024,1024]{1,0:T(8,128)S(1)} %multiply_subtract_fusion.9), kind=kOutput, calls=%fused_computation.28 | convolution fusion | flops 12901679104 | bytes 12582912 | tf_op jit(solution)/shard_map/dot_general | solution.py:11
  765.4 31.3 %subtract_bitcast_fusion = f32[1,1024,1024]{2,1,0:T(8,128)S(1)} fusion(f32[1024,1024]{1,0:T(8,128)S(1)} %fusion.28, f32[1024,1024]{1,0:T(8,128)S(1)} %multiply_add_fusion.9), kind=kOutput, calls=%fused_computation.29 | convolution fusion | flops 12901679104 | bytes 12582912 | tf_op jit(solution)/shard_map/dot_general | solution.py:11
  796.7 4.2 maximum_bitcast_fusion
  800.9 8.7 copy.37
  809.6 9.5 reshape.25
  837.4 1.8 fusion.78
  877.7 187.0 %all_to_all.16 = f32[32,2,1,32768]{3,2,1,0:T(1,128)S(1)} all-to-all(f32[32,2,1,32768]{3,2,1,0:T(1,128)S(1)} %fusion.57), channel_id=1, replica_groups=mesh['hi'=4,'lo'=8] {'hi','lo'}, dimensions={0} | all-to-all | bytes 16777216 | tf_op jit(solution)/shard_map/all_to_all | solution.py:37
  1064.7 7.6 copy.62
  1072.3 22.7 %copy.39 = f32[2,32768,32]{2,1,0:T(8,128)} copy(f32[2,32768,32]{1,0,2:T(2,128)} %bitcast.169) | data formatting | bytes 16777216 | tf_op jit(solution)/shard_map/transpose | solution.py:80
  1095.0 27.8 %reshape.28 = f32[2,1048576]{1,0:T(2,128)} reshape(f32[2,32768,32]{2,1,0:T(8,128)} %copy.39) | data formatting | bytes 16777216 | tf_op jit(solution)/shard_map/reshape | solution.py:80
  (37 shorter events, 57.1 us)
Async XLA Ops:
  0.0 193.4 %all-to-all-start = ((f32[2,32,32768]{2,0,1:T(2,128)}), f32[2,32,32768]{2,0,1:T(2,128)}, u32[]{:S(2)}, u32[]{:S(2)}) async-start(f32[2,32,32768]{2,0,1:T(2,128)} %bitcast.171), calls=%async_computation | async-start | bytes 16777216 | tf_op jit(solution)/shard_map/all_to_all | solution.py:28
  483.7 31.6 %copy-start = (f32[1024,1024]{1,0:T(8,128)S(1)}, f32[1024,1024]{1,0:T(8,128)}, u32[]{:S(2)}) copy-start(f32[1024,1024]{1,0:T(8,128)} %squeeze.18) | copy-start | bytes 12582916
  544.9 29.2 %copy-start.1 = (f32[1024,1024]{1,0:T(8,128)S(1)}, f32[1024,1024]{1,0:T(8,128)}, u32[]{:S(2)}) copy-start(f32[1024,1024]{1,0:T(8,128)} %squeeze.19) | copy-start | bytes 12582916
